TPU v7x, 32 devices: a whole 2x2x4 slice. The times are simulated.
32 devices in a mesh: act: 8 (over z, x), rep: 4 (over y, core).
Axes of the slice: x: 2, y: 2, z: 4, core: 2. Of those that a mesh axis runs over, the one named last changes fastest.
Arguments:
- estimated_returns: float32 [512, 16384], P('act', 'rep'), may hold values from -1000 to 1000
- chosen_move_ids: int32 [512, 16384], P('act', 'rep'), may hold values from 0 to 17
- previous_eta: float32 [1], replicated, may hold values from 0.3 to 3
- trust_region_epsilon: float32 [1], replicated, may hold values from 0.02 to 1
Outputs:
- sample_importance: float32 [512, 16384], P('act', 'rep')
- goal_distribution: float32 [18, 16384], P(None, ('rep', 'act'))
- new_temperature: float32 [1], replicated
All inputs are finite; a program needn't handle non-finite values.
Results may differ from a plain program's by a relative error of at most 0.0003.
Values sent between devices are 32-bit elements; how exact they have to be, the bound alone decides.
A program may use at most 64 MiB of HBM per device.

v0:
```python
import jax
import jax.numpy as jnp
from jax import lax
from jax.sharding import PartitionSpec as P

NACT = 18
ITERS = 3


def summary_figures(centered_returns, lagrange_eta):
    exponential_term = jnp.exp(centered_returns / lagrange_eta)
    partition_total = jnp.sum(exponential_term, axis=0)
    leading_part = jnp.sum(exponential_term * centered_returns, axis=0)
    trailing_part = jnp.sum(exponential_term * centered_returns * centered_returns, axis=0)
    return (exponential_term, partition_total, leading_part, trailing_part)


def within_situation(partition_total, leading_part, trailing_part, lagrange_eta, move_draws):
    entropy_gap = (
        leading_part / (partition_total * lagrange_eta)
        - jnp.log(partition_total)
        + jnp.log(jnp.float32(move_draws))
    )
    mean_first = leading_part / partition_total
    spread = trailing_part / partition_total - mean_first * mean_first
    return (jnp.sum(entropy_gap), jnp.sum(spread))


def gradient_step(lagrange_eta, ceiling_term, aggregate_relative_entropy, aggregate_deviation):
    change_amount = (
        (ceiling_term - aggregate_relative_entropy)
        * lagrange_eta
        / (1.0 + aggregate_deviation / lagrange_eta)
    )
    return lagrange_eta * jnp.exp(-jnp.tanh(change_amount))


def per_action(probs, ids_block):
    return jnp.stack([jnp.sum(jnp.where(ids_block == k, probs, 0.0), axis=0) for k in range(NACT)])


def scatter_target(probs, ids_block):
    return lax.psum_scatter(per_action(probs, ids_block), "act", scatter_dimension=1, tiled=True)


def on_device(estimated_returns, chosen_move_ids, previous_eta, trust_region_epsilon):
    lagrange_eta = previous_eta[0]
    ceiling_term = trust_region_epsilon[0]
    move_draws = estimated_returns.shape[0] * lax.axis_size("act")
    q_rows = lax.all_to_all(estimated_returns, "act", split_axis=1, concat_axis=0, tiled=True)
    tally_number = q_rows.shape[1] * lax.axis_size("act") * lax.axis_size("rep")
    centered_returns = q_rows - jnp.max(q_rows, axis=0, keepdims=True)
    for step in range(ITERS):
        exponential_term, partition_total, leading_part, trailing_part = summary_figures(
            centered_returns, lagrange_eta
        )
        shard_divergence, shard_value_spread = within_situation(
            partition_total, leading_part, trailing_part, lagrange_eta, move_draws
        )
        aggregate_relative_entropy, aggregate_deviation = lax.psum(
            (shard_divergence, shard_value_spread), ("act", "rep")
        )
        lagrange_eta = gradient_step(
            lagrange_eta,
            ceiling_term,
            aggregate_relative_entropy / tally_number,
            aggregate_deviation / tally_number,
        )
    exponential_term, partition_total, leading_part, trailing_part = summary_figures(
        centered_returns, lagrange_eta
    )
    probs_rows = exponential_term / partition_total
    sample_importance = lax.all_to_all(
        move_draws * probs_rows, "act", split_axis=0, concat_axis=1, tiled=True
    )
    goal_distribution = scatter_target(sample_importance / jnp.float32(move_draws), chosen_move_ids)
    return (sample_importance, goal_distribution, jnp.reshape(lagrange_eta, (1,)))


def solution(mesh):
    in_specs = (P("act", "rep"), P("act", "rep"), P(), P())
    out_specs = (P("act", "rep"), P(None, ("rep", "act")), P())
    return jax.shard_map(
        on_device, mesh=mesh, in_specs=in_specs, out_specs=out_specs, check_vma=False
    )
```

profile of v0, /device:TPU:0, one launch (start us, length us, event | category | flops | bytes accessed | tf_op | source)
XLA Modules:
  0.0 275.7 jit_solution(3576206588471246463)
XLA Ops:
  7.2 2.3 copy.12
  9.4 7.3 %all-to-all-start = ((f32[64,8,512]{2,0,1:T(8,128)}), f32[64,8,512]{2,0,1:T(8,128)S(1)}, u32[]{:S(2)}, u32[]{:S(2)}) async-start(f32[64,8,512]{2,0,1:T(8,128)} %bitcast.86), calls=%async_computation | async-start | bytes 2097152 | tf_op jit(solution)/shard_map/all_to_all | solution.py:50
  16.7 0.0 reduce-scatter.2.cloned.1.call-start
  18.1 24.4 %all-to-all-done = f32[64,8,512]{2,0,1:T(8,128)S(1)} async-done(((f32[64,8,512]{2,0,1:T(8,128)}), f32[64,8,512]{2,0,1:T(8,128)S(1)}, u32[]{:S(2)}, u32[]{:S(2)}) %all-to-all-start) | async-done | bytes 1048608 | tf_op jit(solution)/shard_map/all_to_all | solution.py:50
  42.5 0.1 reduce_max.9
  42.6 0.3 fusion.1
  42.9 0.7 subtract_reduce_fusion.2
  43.6 38.0 %all-reduce.2 = (f32[]{:T(128)}, f32[]{:T(128)}) all-reduce(f32[]{:T(128)} %get-tuple-element.35, f32[]{:T(128)} %get-tuple-element.34), channel_id=1, replica_groups=mesh['act'=8,'rep'=4] {'act','rep'}, use_global_device_ids=true, to_apply=%region_4.0 | all-reduce | flops 2 | bytes 16 | tf_op jit(solution)/shard_map/psum | solution.py:60
  83.0 0.3 fusion.3
  83.3 0.6 subtract_reduce_fusion.1
  84.0 41.8 %all-reduce.1 = (f32[]{:T(128)}, f32[]{:T(128)}) all-reduce(f32[]{:T(128)} %get-tuple-element.33, f32[]{:T(128)} %get-tuple-element.32), channel_id=1, replica_groups=mesh['act'=8,'rep'=4] {'act','rep'}, use_global_device_ids=true, to_apply=%region_11.0 | all-reduce | flops 2 | bytes 16 | tf_op jit(solution)/shard_map/psum | solution.py:60
  127.2 0.3 fusion.5
  127.6 0.6 subtract_reduce_fusion
  128.2 39.7 %all-reduce = (f32[]{:T(128)}, f32[]{:T(128)}) all-reduce(f32[]{:T(128)} %get-tuple-element.31, f32[]{:T(128)} %get-tuple-element.30), channel_id=1, replica_groups=mesh['act'=8,'rep'=4] {'act','rep'}, use_global_device_ids=true, to_apply=%region_18.0 | all-reduce | flops 2 | bytes 16 | tf_op jit(solution)/shard_map/psum | solution.py:60
  169.3 0.2 fusion.13
  169.5 0.2 divide_multiply_fusion
  169.8 29.3 %all_to_all.29 = f32[8,64,512]{2,1,0:T(8,128)S(1)} all-to-all(f32[8,64,512]{2,1,0:T(8,128)S(1)} %divide_multiply_fusion), channel_id=1, replica_groups=mesh['act'=8,'rep'=4] {'act'}, dimensions={0} | all-to-all | bytes 2097152 | tf_op jit(solution)/shard_map/all_to_all | solution.py:73
  199.0 0.1 copy.10
  199.1 0.0 copy-start
  199.1 1.5 copy-done.1
  200.6 2.7 select_reduce_fusion
  203.4 2.4 stack.75
  205.7 0.0 reduce-scatter.2.cloned.1.call-update
  205.8 62.0 %reduce-scatter.2.cloned.1.call-done = f32[18,512]{1,0:T(8,128)} async-done(((f32[18,4096]{1,0:T(8,128)}), f32[18,512]{1,0:T(8,128)}) %reduce-scatter.2.cloned.1.call-update) | async-done | bytes 36880 | tf_op jit(solution)/shard_map/reduce_scatter | solution.py:43
  (2 shorter events, 0.0 us)
Async XLA Ops:
  9.4 33.0 %all-to-all-start = ((f32[64,8,512]{2,0,1:T(8,128)}), f32[64,8,512]{2,0,1:T(8,128)S(1)}, u32[]{:S(2)}, u32[]{:S(2)}) async-start(f32[64,8,512]{2,0,1:T(8,128)} %bitcast.86), calls=%async_computation | async-start | bytes 2097152 | tf_op jit(solution)/shard_map/all_to_all | solution.py:50
  16.7 251.0 %reduce-scatter.2.cloned.1.call-start = ((), (), s32[]{:S(2)}) async-start(), calls=%async_computation.3 | async-start | bytes 442368 | tf_op jit(solution)/shard_map/reduce_scatter | solution.py:43
  199.0 1.6 copy-start.1
  199.1 4.2 %copy-start = (f32[8,8,8,512]{3,2,0,1:T(8,128)}, f32[8,8,8,512]{3,2,0,1:T(8,128)S(1)}, u32[]{:S(2)}) copy-start(f32[8,8,8,512]{3,2,0,1:T(8,128)S(1)} %copy.10) | copy-start | bytes 3145732
Sparse Core Ops, SparseCore 0:
  205.9 61.8 reduce-scatter.1
where the time goes:
time: 277 us; the launch traced here: 276 us
  blocking collectives  149 us (54%)
  waiting for transfers between devices  86.4 us (31%)
  between operations  20.8 us (8%)
  starting transfers between devices  7.32 us (3%)
  local copies, waits for them, and re-layouts  6.25 us (2%)
  other arithmetic  6.15 us (2%)
    psum x3, blocking collectives, on_device(): lax.psum((shard_divergence, shard_value_spread), ('act', 'rep'))  119 us
    reduce_scatter x1, waiting for transfers between devices, scatter_target(): lax.psum_scatter(per_action(probs, ids_block), 'act', scatter_dimension=1...  62 us
    all_to_all x1, blocking collectives, on_device(): lax.all_to_all(move_draws * probs_rows, 'act', split_axis=0, concat_axis=...  29.3 us
    all_to_all x1, waiting for transfers between devices, on_device(): lax.all_to_all(estimated_returns, 'act', split_axis=1, concat_axis=0, til...  24.4 us
    all_to_all x1, starting transfers between devices, on_device(): lax.all_to_all(estimated_returns, 'act', split_axis=1, concat_axis=0, til...  7.28 us
  transfers between devices with their start and end apart: 2, of which 2 were waited for; matrix products, arithmetic and copies ran while one was open for 0% of the time, Pallas kernels for 0%

commit v1 on v0

v1 whole, which is shorter than its diff:
```python
import functools

import jax
import jax.numpy as jnp
from jax import lax
from jax.experimental import pallas as pl
from jax.experimental.pallas import tpu as pltpu
from jax.sharding import PartitionSpec as P

NACT = 18
ITERS = 3
LANES = 128
MESH = pl.DeviceIdType.MESH


def fold_lanes(x):
    total = x[:, :LANES]
    for i in range(1, x.shape[1] // LANES):
        total = total + x[:, i * LANES : (i + 1) * LANES]
    return total


def kernel(
    n, m, q_hbm, ids_hbm, eta_ref, eps_ref,
    expo_hbm, scale_ref, goal_ref, eta_out,
    q, ids, stat_src, stat_dst, pair_src, pair_dst, z_src, z_dst, goal_src, goal_dst, scale_src, scale_dst, delta,
    local_sem, stat_send, stat_recv, pair_send, pair_recv, z_sem, goal_sem, scale_sem,
):
    a, r = lax.axis_index("act"), lax.axis_index("rep")
    me = r * n + a
    devices = n * m
    rows, columns = q.shape
    width = columns // n
    samples = jnp.float32(rows * n)
    states = jnp.float32(columns * m)

    barrier = pltpu.get_barrier_semaphore()

    def greet(o, c):
        to = lax.rem(me + o, devices)
        pl.semaphore_signal(
            barrier, inc=1, device_id={"act": lax.rem(to, n), "rep": to // n}, device_id_type=MESH
        )
        return c

    lax.fori_loop(1, devices, greet, 0)
    load_q = pltpu.make_async_copy(q_hbm, q, local_sem.at[0])
    load_ids = pltpu.make_async_copy(ids_hbm, ids, local_sem.at[1])
    load_q.start()
    load_ids.start()
    load_q.wait()

    def cols(j):
        return pl.ds(pl.multiple_of(j * width, LANES), width)

    def to_peer(src, dst, send, recv, j):
        return pltpu.make_async_remote_copy(
            src_ref=src, dst_ref=dst, send_sem=send, recv_sem=recv,
            device_id={"act": j, "rep": r}, device_id_type=MESH,
        )

    def all_but_one(ref, count, sem):
        some = ref.at[pl.ds(0, count - 1)]
        pltpu.make_async_copy(some, some, sem).wait()

    eta = jnp.full((1, LANES), eta_ref[0], jnp.float32)
    eps = jnp.full((1, LANES), eps_ref[0], jnp.float32)

    def statistics(step, j, inverse):
        c = cols(j)
        if step == 0:
            block = q[:, c]
            top = jnp.max(block, axis=0, keepdims=True)
            shifted = block - top
            q[:, c] = shifted
            stat_src[step, j, 3:4, :] = top
        else:
            shifted = q[:, c]
        expo = jnp.exp(shifted * inverse)
        first = expo * shifted
        stat_src[step, j, 0:1, :] = jnp.sum(expo, axis=0, keepdims=True)
        stat_src[step, j, 1:2, :] = jnp.sum(first, axis=0, keepdims=True)
        stat_src[step, j, 2:3, :] = jnp.sum(first * shifted, axis=0, keepdims=True)

    for step in range(ITERS):
        inverse = 1.0 / eta[:, :1]
        if step == 0:
            lax.fori_loop(0, n, lambda o, c: (statistics(0, o, inverse), c)[1], 0)
            pl.semaphore_wait(barrier, devices - 1)

        def send(o, c):
            j = lax.rem(a + o, n)
            if step > 0:
                statistics(step, j, inverse)
            to_peer(
                stat_src.at[step, j], stat_dst.at[step, a], stat_send.at[step], stat_recv.at[step], j
            ).start()
            return c

        lax.fori_loop(1, n, send, 0)
        if step > 0:
            statistics(step, a, inverse)
        stat_dst[step, a] = stat_src[step, a]
        all_but_one(stat_dst.at[step], n, stat_recv.at[step])
        z_d = stat_dst[step, :, 0, :]
        c1_d = stat_dst[step, :, 1, :]
        c2_d = stat_dst[step, :, 2, :]
        if step == 0:
            top_d = stat_dst[step, :, 3, :]
            gap = top_d - jnp.max(top_d, axis=0, keepdims=True)
            delta[...] = gap
        else:
            gap = delta[...]
        e_d = jnp.exp(gap * inverse)
        z = jnp.sum(e_d * z_d, axis=0, keepdims=True)
        c1 = jnp.sum(e_d * (c1_d + gap * z_d), axis=0, keepdims=True)
        c2 = jnp.sum(e_d * (c2_d + gap * (2.0 * c1_d + gap * z_d)), axis=0, keepdims=True)
        mean = c1 / z
        kl = mean * inverse - jnp.log(z) + jnp.log(samples)
        spread = c2 / z - mean * mean
        pair_src[step, 0:1, :] = fold_lanes(kl)
        pair_src[step, 1:2, :] = fold_lanes(spread)

        def share(o, c):
            to = lax.rem(me + o, devices)
            pltpu.make_async_remote_copy(
                src_ref=pair_src.at[step], dst_ref=pair_dst.at[step, me],
                send_sem=pair_send.at[step], recv_sem=pair_recv.at[step],
                device_id={"act": lax.rem(to, n), "rep": to // n}, device_id_type=MESH,
            ).start()
            return c

        lax.fori_loop(1, devices, share, 0)
        pair_dst[step, me] = pair_src[step]
        all_but_one(pair_dst.at[step], devices, pair_recv.at[step])
        both = jnp.sum(pair_dst[step], axis=0)
        both = jnp.sum(both, axis=1, keepdims=True) / states
        k_mean = jnp.broadcast_to(both[0:1], (1, LANES))
        v_mean = jnp.broadcast_to(both[1:2], (1, LANES))
        change = (eps - k_mean) * eta / (1.0 + v_mean / eta)
        eta = eta * jnp.exp(-jnp.tanh(change))

    inverse = 1.0 / eta[:, :1]
    eta_out[...] = eta

    def weights(j):
        c = cols(j)
        expo = jnp.exp(q[:, c] * inverse)
        q[:, c] = expo
        z_src[j] = jnp.sum(expo, axis=0, keepdims=True)

    def send_z(o, c):
        j = lax.rem(a + o, n)
        weights(j)
        to_peer(z_src.at[j], z_dst.at[a], z_sem.at[0], z_sem.at[1], j).start()
        return c

    lax.fori_loop(1, n, send_z, 0)
    weights(a)
    z_dst[a] = z_src[a]
    store_expo = pltpu.make_async_copy(q, expo_hbm, local_sem.at[2])
    store_expo.start()
    load_ids.wait()

    def goals(j):
        c = cols(j)
        for i in range(width // LANES):
            sub = pl.ds(pl.multiple_of(j * width + i * LANES, LANES), LANES)
            expo, moves = q[:, sub], ids[:, sub]
            for k in range(NACT):
                goal_src[j, k : k + 1, i * LANES : (i + 1) * LANES] = jnp.sum(
                    jnp.where(moves == k, expo, 0.0), axis=0, keepdims=True
                )

    def send_goals(o, c):
        j = lax.rem(a + o, n)
        goals(j)
        to_peer(goal_src.at[j], goal_dst.at[a], goal_sem.at[0], goal_sem.at[1], j).start()
        return c

    lax.fori_loop(1, n, send_goals, 0)
    goals(a)
    goal_dst[a] = goal_src[a]

    all_but_one(z_dst, n, z_sem.at[1])
    e_d = jnp.exp(delta[...] * inverse)
    z = jnp.sum(e_d * z_dst[:, 0, :], axis=0, keepdims=True)
    part = e_d / z
    delta[...] = part
    scale_src[:, 0, :] = samples * part

    def send_scale(o, c):
        j = lax.rem(a + o, n)
        to_peer(scale_src.at[j], scale_dst.at[a], scale_sem.at[0], scale_sem.at[1], j).start()
        return c

    lax.fori_loop(1, n, send_scale, 0)
    scale_dst[a] = scale_src[a]
    all_but_one(goal_dst, n, goal_sem.at[1])
    goal_ref[...] = lax.fori_loop(
        0, n, lambda d, t: t + delta[pl.ds(d, 1), :] * goal_dst[d], jnp.zeros((NACT, width), jnp.float32)
    )
    all_but_one(scale_dst, n, scale_sem.at[1])

    def place(j, c):
        scale_ref[:, cols(j)] = scale_dst[j]
        return c

    lax.fori_loop(0, n, place, 0)
    for step in range(ITERS):
        all_but_one(stat_src.at[step], n, stat_send.at[step])
        some = pair_dst.at[step, pl.ds(0, devices - 1)]
        pltpu.make_async_copy(some, some, pair_send.at[step]).wait()
    all_but_one(z_src, n, z_sem.at[0])
    all_but_one(goal_src, n, goal_sem.at[0])
    all_but_one(scale_src, n, scale_sem.at[0])
    store_expo.wait()


def on_device(n, m, estimated_returns, chosen_move_ids, previous_eta, trust_region_epsilon):
    rows, columns = estimated_returns.shape
    width = columns // n
    f32 = jnp.float32
    anywhere = pl.BlockSpec(memory_space=pl.ANY)
    vmem = pl.BlockSpec(memory_space=pltpu.VMEM)
    smem = pl.BlockSpec(memory_space=pltpu.SMEM)
    dma = pltpu.SemaphoreType.DMA
    expo, scale, goal, eta = pl.pallas_call(
        functools.partial(kernel, n, m),
        name="dual",
        out_shape=(
            jax.ShapeDtypeStruct((rows, columns), f32),
            jax.ShapeDtypeStruct((1, columns), f32),
            jax.ShapeDtypeStruct((NACT, width), f32),
            jax.ShapeDtypeStruct((1, LANES), f32),
        ),
        in_specs=[anywhere, anywhere, smem, smem],
        out_specs=(anywhere, vmem, vmem, vmem),
        scratch_shapes=[
            pltpu.VMEM((rows, columns), f32),
            pltpu.VMEM((rows, columns), jnp.int32),
            pltpu.VMEM((ITERS, n, 4, width), f32),
            pltpu.VMEM((ITERS, n, 4, width), f32),
            pltpu.VMEM((ITERS, 2, LANES), f32),
            pltpu.VMEM((ITERS, n * m, 2, LANES), f32),
            pltpu.VMEM((n, 1, width), f32),
            pltpu.VMEM((n, 1, width), f32),
            pltpu.VMEM((n, NACT, width), f32),
            pltpu.VMEM((n, NACT, width), f32),
            pltpu.VMEM((n, 1, width), f32),
            pltpu.VMEM((n, 1, width), f32),
            pltpu.VMEM((n, width), f32),
            dma((3,)), dma((ITERS,)), dma((ITERS,)), dma((ITERS,)), dma((ITERS,)), dma((2,)), dma((2,)), dma((2,)),
        ],
        compiler_params=pltpu.CompilerParams(collective_id=0, has_side_effects=True),
    )(estimated_returns, chosen_move_ids, previous_eta, trust_region_epsilon)
    return expo * scale, goal, eta[0, :1]


def solution(mesh):
    n, m = mesh.shape["act"], mesh.shape["rep"]
    return jax.shard_map(
        functools.partial(on_device, n, m),
        mesh=mesh,
        in_specs=(P("act", "rep"), P("act", "rep"), P(), P()),
        out_specs=(P("act", "rep"), P(None, ("rep", "act")), P()),
        check_vma=False,
    )
```

time: 277 us -> 54 us (0.19)
  blocking collectives: 149 us -> 0 us
  waiting for transfers between devices: 86.4 us -> 0 us
  Pallas kernels: 0 us -> 47.8 us
  between operations: 20.8 us -> 3.11 us
  starting transfers between devices: 7.32 us -> 0 us
  local copies, waits for them, and re-layouts: 6.25 us -> 0.63 us
  other arithmetic: 6.15 us -> 2.29 us
    psum x3 -> x0, blocking collectives: 119 us -> none  [on_device(): lax.psum((shard_divergence, shard_value_spread), ('act', 'rep'))]
    reduce_scatter x1 -> x0, waiting for transfers between devices: 62 us -> none  [scatter_target(): lax.psum_scatter(per_action(probs, ids_block), 'act', scatter_dimension=1...]
    pallas_call x0 -> x1, Pallas kernels: none -> 47.8 us  [on_device(): pl.pallas_call(functools.partial(kernel, n, m), name='dual', out_shape=(j...]
    all_to_all x1 -> x0, blocking collectives: 29.3 us -> none  [on_device(): lax.all_to_all(move_draws * probs_rows, 'act', split_axis=0, concat_axis=...]
    all_to_all x1 -> x0, waiting for transfers between devices: 24.4 us -> none  [on_device(): lax.all_to_all(estimated_returns, 'act', split_axis=1, concat_axis=0, til...]
    all_to_all x1 -> x0, starting transfers between devices: 7.28 us -> none  [on_device(): lax.all_to_all(estimated_returns, 'act', split_axis=1, concat_axis=0, til...]
    reduce_sum x8 -> x0, other arithmetic: 5.83 us -> none  [the longest x1 2.71 us: per_action(): jnp.sum(jnp.where(ids_block == k, probs, 0.0), axis=0)]
  transfers between devices with their start and end apart: 2 -> 0, of which waited for: 2 -> 0; matrix products, arithmetic and copies ran while one was open for 0% -> 0% of each run, Pallas kernels for 0% -> 0%
where the time goes in v1:
time: 54 us; the launch traced here: 53.8 us
  Pallas kernels  47.8 us (89%)
  between operations  3.11 us (6%)
  other arithmetic  2.29 us (4%)
  local copies, waits for them, and re-layouts  0.63 us (1%)
    pallas_call x1, Pallas kernels, on_device(): pl.pallas_call(functools.partial(kernel, n, m), name='dual', out_shape=(j...  47.8 us
    mul x1, other arithmetic, on_device(): return (expo * scale, goal, eta[0, :1])  2.29 us

profile of v1, /device:TPU:0, one launch (start us, length us, event | category | flops | bytes accessed | tf_op | source)
XLA Modules:
  0.0 53.8 jit_solution(2917843765985978214)
XLA Ops:
  1.9 47.8 %dual.1 = (f32[64,4096]{1,0:T(8,128)}, f32[1,4096]{1,0:T(1,128)}, f32[18,512]{1,0:T(8,128)}, f32[1,128]{1,0:T(1,128)}) custom-call(f32[64,4096]{1,0:T(8,128)} %q_hbm.1, s32[64,4096]{1,0:T(8,128)} %ids_hbm.1, f32[1]{0:T(128)S(6)} %copy.9.eta_ref, f32[1]{0:T(128)S(6)} %copy.10.eps_ref), custom_call_target="tpu_custom_call" | custom-call | tf_op jit(solution)/shard_map/dual/pallas_call | solution.py:228
  49.7 0.0 copy-start
  49.7 2.3 %broadcast_multiply_fusion = f32[64,4096]{1,0:T(8,128)} fusion(f32[64,4096]{1,0:T(8,128)} %get-tuple-element.7, f32[4096]{0:T(1024)} %bitcast.3), kind=kLoop, calls=%fused_computation | loop fusion | flops 262144 | bytes 2113536 | tf_op jit(solution)/shard_map/mul | solution.py:257
  52.0 0.0 copy-done
  52.0 0.0 copy-start.1
  52.0 0.6 %copy.11 = f32[18,512]{1,0:T(8,128)} copy(f32[18,512]{1,0:T(8,128)S(1)} %copy-done) | data formatting | bytes 73728
  52.6 0.0 copy-done.1
Async XLA Ops:
  49.7 2.3 %copy-start = (f32[18,512]{1,0:T(8,128)S(1)}, f32[18,512]{1,0:T(8,128)}, u32[]{:S(2)}) copy-start(f32[18,512]{1,0:T(8,128)} %get-tuple-element.15) | copy-start | bytes 110596
  52.0 0.6 %copy-start.1 = (f32[1,128]{1,0:T(1,128)S(1)}, f32[1,128]{1,0:T(1,128)}, u32[]{:S(2)}) copy-start(f32[1,128]{1,0:T(1,128)} %get-tuple-element.10) | copy-start | bytes 1540

commit v2 on v1

v2 whole, which is shorter than its diff:
```python
import functools

import jax
import jax.numpy as jnp
from jax import lax
from jax.experimental import pallas as pl
from jax.experimental.pallas import tpu as pltpu
from jax.sharding import PartitionSpec as P

NACT = 18
ITERS = 3
LANES = 128
MESH = pl.DeviceIdType.MESH


def fold_lanes(x):
    total = x[:, :LANES]
    for i in range(1, x.shape[1] // LANES):
        total = total + x[:, i * LANES : (i + 1) * LANES]
    return total


def kernel(
    n, m, q_hbm, ids_hbm, eta_ref, eps_ref,
    expo_hbm, scale_ref, goal_ref, eta_out,
    q, ids, stat_src, stat_dst, pair_src, pair_dst, pair_sent, z_src, z_dst, goal_src, goal_dst, scale_src, scale_dst, delta, parts,
    local_sem, stat_send, stat_recv, pair_send, pair_recv, z_sem, goal_sem, scale_sem,
):
    a, r = lax.axis_index("act"), lax.axis_index("rep")
    me = r * n + a
    devices = n * m
    rows, columns = q.shape
    width = columns // n
    owners, first_owner = n // 2, n // 4
    wide = columns // owners
    is_owner = jnp.logical_and(a >= first_owner, a < first_owner + owners)
    mine = lax.rem(a - first_owner + n, n)
    samples = jnp.float32(rows * n)
    states = jnp.float32(columns * m)

    barrier = pltpu.get_barrier_semaphore()

    def greet(o, c):
        to = lax.rem(me + o, devices)
        pl.semaphore_signal(
            barrier, inc=1, device_id={"act": lax.rem(to, n), "rep": to // n}, device_id_type=MESH
        )
        return c

    lax.fori_loop(1, devices, greet, 0)
    load_q = pltpu.make_async_copy(q_hbm, q, local_sem.at[0])
    load_ids = pltpu.make_async_copy(ids_hbm, ids, local_sem.at[1])
    load_q.start()
    load_ids.start()
    load_q.wait()

    def wide_cols(i):
        return pl.ds(pl.multiple_of(i * wide, LANES), wide)

    def cols(j):
        return pl.ds(pl.multiple_of(j * width, LANES), width)

    def to_peer(src, dst, send, recv, j):
        return pltpu.make_async_remote_copy(
            src_ref=src, dst_ref=dst, send_sem=send, recv_sem=recv,
            device_id={"act": j, "rep": r}, device_id_type=MESH,
        )

    def all_but_one(ref, count, sem):
        some = ref.at[pl.ds(0, count - 1)]
        pltpu.make_async_copy(some, some, sem).wait()

    eta = jnp.full((1, LANES), eta_ref[0], jnp.float32)
    eps = jnp.full((1, LANES), eps_ref[0], jnp.float32)

    def statistics(step, i, inverse):
        c = wide_cols(i)
        if step == 0:
            block = q[:, c]
            top = jnp.max(block, axis=0, keepdims=True)
            shifted = block - top
            q[:, c] = shifted
            stat_src[step, i, 3:4, :] = top
        else:
            shifted = q[:, c]
        expo = jnp.exp(shifted * inverse)
        first = expo * shifted
        stat_src[step, i, 0:1, :] = jnp.sum(expo, axis=0, keepdims=True)
        stat_src[step, i, 1:2, :] = jnp.sum(first, axis=0, keepdims=True)
        stat_src[step, i, 2:3, :] = jnp.sum(first * shifted, axis=0, keepdims=True)

    for step in range(ITERS):
        inverse = 1.0 / eta[:, :1]
        if step == 0:
            lax.fori_loop(0, owners, lambda i, c: (statistics(0, i, inverse), c)[1], 0)
            pl.semaphore_wait(barrier, devices - 1)

        def send(o, c):
            i = lax.rem(a - first_owner + n // 2 + o + n, owners)
            if step > 0:
                statistics(step, i, inverse)

            @pl.when(i + first_owner != a)
            def _():
                to_peer(
                    stat_src.at[step, i], stat_dst.at[step, a], stat_send.at[step], stat_recv.at[step],
                    i + first_owner,
                ).start()

            return c

        lax.fori_loop(0, owners, send, 0)

        @pl.when(is_owner)
        def _():
            stat_dst[step, a] = stat_src[step, mine]
            all_but_one(stat_dst.at[step], n, stat_recv.at[step])
            z_d = stat_dst[step, :, 0, :]
            c1_d = stat_dst[step, :, 1, :]
            c2_d = stat_dst[step, :, 2, :]
            if step == 0:
                top_d = stat_dst[step, :, 3, :]
                gap = top_d - jnp.max(top_d, axis=0, keepdims=True)
                delta[...] = gap
            else:
                gap = delta[...]
            e_d = jnp.exp(gap * inverse)
            z = jnp.sum(e_d * z_d, axis=0, keepdims=True)
            c1 = jnp.sum(e_d * (c1_d + gap * z_d), axis=0, keepdims=True)
            c2 = jnp.sum(e_d * (c2_d + gap * (2.0 * c1_d + gap * z_d)), axis=0, keepdims=True)
            mean = c1 / z
            kl = mean * inverse - jnp.log(z) + jnp.log(samples)
            spread = c2 / z - mean * mean
            pair_src[step, 0:1, :] = fold_lanes(kl)
            pair_src[step, 1:2, :] = fold_lanes(spread)
            slot = r * owners + mine

            def share(o, c):
                to = lax.rem(me + o, devices)
                pltpu.make_async_remote_copy(
                    src_ref=pair_src.at[step], dst_ref=pair_dst.at[step, slot],
                    send_sem=pair_send.at[step], recv_sem=pair_recv.at[step],
                    device_id={"act": lax.rem(to, n), "rep": to // n}, device_id_type=MESH,
                ).start()
                return c

            lax.fori_loop(1, devices, share, 0)
            pair_dst[step, slot] = pair_src[step]
            all_but_one(pair_dst.at[step], owners * m, pair_recv.at[step])

        @pl.when(jnp.logical_not(is_owner))
        def _():
            pltpu.make_async_copy(pair_dst.at[step], pair_dst.at[step], pair_recv.at[step]).wait()

        both = jnp.sum(pair_dst[step], axis=0)
        both = jnp.sum(both, axis=1, keepdims=True) / states
        k_mean = jnp.broadcast_to(both[0:1], (1, LANES))
        v_mean = jnp.broadcast_to(both[1:2], (1, LANES))
        change = (eps - k_mean) * eta / (1.0 + v_mean / eta)
        eta = eta * jnp.exp(-jnp.tanh(change))

    inverse = 1.0 / eta[:, :1]
    eta_out[...] = eta

    def weights(j):
        c = cols(j)
        expo = jnp.exp(q[:, c] * inverse)
        q[:, c] = expo
        z_src[j, 0:1, :] = jnp.sum(expo, axis=0, keepdims=True)
        z_src[j, 1:2, :] = stat_src[0, j * width // wide, 3:4, pl.ds(pl.multiple_of(lax.rem(j * width, wide), LANES), width)]

    def send_z(o, c):
        j = lax.rem(a + o, n)
        weights(j)
        to_peer(z_src.at[j], z_dst.at[a], z_sem.at[0], z_sem.at[1], j).start()
        return c

    lax.fori_loop(1, n, send_z, 0)
    weights(a)
    z_dst[a] = z_src[a]
    store_expo = pltpu.make_async_copy(q, expo_hbm, local_sem.at[2])
    store_expo.start()
    load_ids.wait()

    def goals(j):
        c = cols(j)
        for i in range(width // LANES):
            sub = pl.ds(pl.multiple_of(j * width + i * LANES, LANES), LANES)
            expo, moves = q[:, sub], ids[:, sub]
            for k in range(NACT):
                goal_src[j, k : k + 1, i * LANES : (i + 1) * LANES] = jnp.sum(
                    jnp.where(moves == k, expo, 0.0), axis=0, keepdims=True
                )

    def start_goals(o, c):
        j = lax.rem(a + o, n)
        to_peer(goal_src.at[j], goal_dst.at[a], goal_sem.at[0], goal_sem.at[1], j).start()
        return c

    def send_goals(o, c):
        goals(lax.rem(a + o, n))
        return start_goals(o, c)

    lax.fori_loop(1, n // 2, send_goals, 0)
    lax.fori_loop(n // 2, n + 1, lambda o, c: (goals(lax.rem(a + o, n)), c)[1], 0)
    goal_dst[a] = goal_src[a]

    all_but_one(z_dst, n, z_sem.at[1])
    top_d = z_dst[:, 1, :]
    e_d = jnp.exp((top_d - jnp.max(top_d, axis=0, keepdims=True)) * inverse)
    z = jnp.sum(e_d * z_dst[:, 0, :], axis=0, keepdims=True)
    part = e_d / z
    parts[...] = part
    scale_src[:, 0, :] = samples * part

    def send_scale(o, c):
        j = lax.rem(a + o, n)
        to_peer(scale_src.at[j], scale_dst.at[a], scale_sem.at[0], scale_sem.at[1], j).start()
        return c

    lax.fori_loop(1, n, send_scale, 0)
    lax.fori_loop(n // 2, n, start_goals, 0)
    scale_dst[a] = scale_src[a]
    all_but_one(goal_dst, n, goal_sem.at[1])
    goal_ref[...] = lax.fori_loop(
        0, n, lambda d, t: t + parts[pl.ds(d, 1), :] * goal_dst[d], jnp.zeros((NACT, width), jnp.float32)
    )
    all_but_one(scale_dst, n, scale_sem.at[1])

    def place(j, c):
        scale_ref[:, cols(j)] = scale_dst[j]
        return c

    lax.fori_loop(0, n, place, 0)
    for step in range(ITERS):

        @pl.when(is_owner)
        def _():
            all_but_one(stat_src.at[step], owners, stat_send.at[step])
            some = pair_sent.at[pl.ds(0, devices - 1)]
            pltpu.make_async_copy(some, some, pair_send.at[step]).wait()

        @pl.when(jnp.logical_not(is_owner))
        def _():
            pltpu.make_async_copy(stat_src.at[step], stat_src.at[step], stat_send.at[step]).wait()

    all_but_one(z_src, n, z_sem.at[0])
    all_but_one(goal_src, n, goal_sem.at[0])
    all_but_one(scale_src, n, scale_sem.at[0])
    store_expo.wait()


def finish(expo_ref, scale_ref, goal_ref, eta_ref, sample_hbm, goal_hbm, eta_hbm, sample, sem):
    rows, columns = sample.shape
    pieces = sem.shape[0] - 2
    tall = rows // pieces
    copies = [
        pltpu.make_async_copy(goal_ref, goal_hbm, sem.at[pieces]),
        pltpu.make_async_copy(eta_ref, eta_hbm, sem.at[pieces + 1]),
    ]
    for copy in copies:
        copy.start()
    for i in range(pieces):
        at = pl.ds(i * tall, tall)
        sample[at, :] = expo_ref[at, :] * scale_ref[...]
        copy = pltpu.make_async_copy(sample.at[at], sample_hbm.at[at], sem.at[i])
        copy.start()
        copies.append(copy)
    for copy in copies:
        copy.wait()


def on_device(n, m, estimated_returns, chosen_move_ids, previous_eta, trust_region_epsilon):
    rows, columns = estimated_returns.shape
    width = columns // n
    owners = n // 2
    wide = columns // owners
    f32 = jnp.float32
    anywhere = pl.BlockSpec(memory_space=pl.ANY)
    vmem = pl.BlockSpec(memory_space=pltpu.VMEM)
    smem = pl.BlockSpec(memory_space=pltpu.SMEM)
    dma = pltpu.SemaphoreType.DMA
    expo, scale, goal, eta = pl.pallas_call(
        functools.partial(kernel, n, m),
        name="dual",
        out_shape=(
            jax.ShapeDtypeStruct((rows, columns), f32),
            jax.ShapeDtypeStruct((1, columns), f32),
            jax.ShapeDtypeStruct((NACT, width), f32),
            jax.ShapeDtypeStruct((1, LANES), f32),
        ),
        in_specs=[anywhere, anywhere, smem, smem],
        out_specs=(anywhere, vmem, vmem, vmem),
        scratch_shapes=[
            pltpu.VMEM((rows, columns), f32),
            pltpu.VMEM((rows, columns), jnp.int32),
            pltpu.VMEM((ITERS, owners, 4, wide), f32),
            pltpu.VMEM((ITERS, n, 4, wide), f32),
            pltpu.VMEM((ITERS, 2, LANES), f32),
            pltpu.VMEM((ITERS, owners * m, 2, LANES), f32),
            pltpu.VMEM((n * m, 2, LANES), f32),
            pltpu.VMEM((n, 2, width), f32),
            pltpu.VMEM((n, 2, width), f32),
            pltpu.VMEM((n, NACT, width), f32),
            pltpu.VMEM((n, NACT, width), f32),
            pltpu.VMEM((n, 1, width), f32),
            pltpu.VMEM((n, 1, width), f32),
            pltpu.VMEM((n, wide), f32),
            pltpu.VMEM((n, width), f32),
            dma((3,)), dma((ITERS,)), dma((ITERS,)), dma((ITERS,)), dma((ITERS,)), dma((2,)), dma((2,)), dma((2,)),
        ],
        compiler_params=pltpu.CompilerParams(collective_id=0, has_side_effects=True, vmem_limit_bytes=24*2**20),
    )(estimated_returns, chosen_move_ids, previous_eta, trust_region_epsilon)
    pieces = max(rows // 8, 1)
    sample, goal, eta = pl.pallas_call(
        finish,
        name="finish",
        out_shape=(
            jax.ShapeDtypeStruct((rows, columns), f32),
            jax.ShapeDtypeStruct((NACT, width), f32),
            jax.ShapeDtypeStruct((1, LANES), f32),
        ),
        in_specs=[vmem, vmem, vmem, vmem],
        out_specs=(anywhere, anywhere, anywhere),
        scratch_shapes=[pltpu.VMEM((rows, columns), f32), dma((pieces + 2,))],
        compiler_params=pltpu.CompilerParams(vmem_limit_bytes=32 * 2**20),
    )(expo, scale, goal, eta)
    return sample, goal, eta[0, :1]


def solution(mesh):
    n, m = mesh.shape["act"], mesh.shape["rep"]
    return jax.shard_map(
        functools.partial(on_device, n, m),
        mesh=mesh,
        in_specs=(P("act", "rep"), P("act", "rep"), P(), P()),
        out_specs=(P("act", "rep"), P(None, ("rep", "act")), P()),
        check_vma=False,
    )
```

time: 54 us -> 48.6 us (0.900)
  Pallas kernels: 47.8 us -> 44 us
  other arithmetic: 2.29 us -> 0 us
  local copies, waits for them, and re-layouts: 0.63 us -> 2.44 us
  between operations: 3.11 us -> 1.94 us
    pallas_call x1, Pallas kernels: 47.8 us -> 42.9 us  [on_device(): pl.pallas_call(functools.partial(kernel, n, m), name='dual', out_shape=(j...]
    mul x1 -> x0, other arithmetic: 2.29 us -> none  [on_device(): return (expo * scale, goal, eta[0, :1])]
    unnamed x5 -> x4, local copies, waits for them, and re-layouts: 0.63 us -> 2.44 us
    pallas_call x0 -> x1, Pallas kernels: none -> 1.07 us  [on_device(): pl.pallas_call(finish, name='finish', out_shape=(jax.ShapeDtypeStruct((ro...]
where the time goes in v2:
time: 48.6 us; the launch traced here: 48.4 us
  Pallas kernels  44 us (91%)
  local copies, waits for them, and re-layouts  2.44 us (5%)
  between operations  1.94 us (4%)
    pallas_call x1, Pallas kernels, on_device(): pl.pallas_call(functools.partial(kernel, n, m), name='dual', out_shape=(j...  42.9 us
    unnamed x4, local copies, waits for them, and re-layouts  2.44 us
    pallas_call x1, Pallas kernels, on_device(): pl.pallas_call(finish, name='finish', out_shape=(jax.ShapeDtypeStruct((ro...  1.07 us

profile of v2, /device:TPU:0, one launch (start us, length us, event | category | flops | bytes accessed | tf_op | source)
XLA Modules:
  0.0 48.4 jit_solution(15358623401230149424)
XLA Ops:
  1.9 0.0 copy-start
  1.9 1.2 %copy-done = f32[64,4096]{1,0:T(8,128)S(1)} copy-done((f32[64,4096]{1,0:T(8,128)S(1)}, f32[64,4096]{1,0:T(8,128)}, u32[]{:S(2)}) %copy-start) | copy-done | bytes 1048600
  3.1 0.0 copy-start.1
  3.1 1.2 %copy-done.1 = s32[64,4096]{1,0:T(8,128)S(1)} copy-done((s32[64,4096]{1,0:T(8,128)S(1)}, s32[64,4096]{1,0:T(8,128)}, u32[]{:S(2)}) %copy-start.1) | copy-done | bytes 1048600
  4.4 42.9 %dual.1 = (f32[64,4096]{1,0:T(8,128)S(1)}, f32[1,4096]{1,0:T(1,128)S(1)}, f32[18,512]{1,0:T(8,128)S(1)}, f32[1,128]{1,0:T(1,128)S(1)}) custom-call(f32[64,4096]{1,0:T(8,128)S(1)} %copy-done, s32[64,4096]{1,0:T(8,128)S(1)} %copy-done.1, f32[1]{0:T(128)S(6)} %copy.7.eta_ref, f32[1]{0:T(128)S(6)} %copy.8.eps_ref), custom_call_target="tpu_custom_call" | custom-call | tf_op jit(solution)/shard_map/dual/pallas_call | solution.py:283
  47.3 1.1 %finish.1 = (f32[64,4096]{1,0:T(8,128)}, f32[18,512]{1,0:T(8,128)}, f32[1,128]{1,0:T(1,128)}) custom-call(f32[64,4096]{1,0:T(8,128)S(1)} %get-tuple-element.10.expo_ref, f32[1,4096]{1,0:T(1,128)S(1)} %get-tuple-element.11.scale_ref, f32[18,512]{1,0:T(8,128)S(1)} %get-tuple-element.12.goal_ref, f32[1,128]{1,0:T(1,128)S(1)} %get-tuple-element.13.eta_ref), custom_call_target="tpu_custom_call" | custom-call | tf_op jit(solution)/shard_map/finish/pallas_call | solution.py:315
Async XLA Ops:
  1.9 1.2 %copy-start = (f32[64,4096]{1,0:T(8,128)S(1)}, f32[64,4096]{1,0:T(8,128)}, u32[]{:S(2)}) copy-start(f32[64,4096]{1,0:T(8,128)} %q_hbm.1) | copy-start | bytes 3145732
  3.1 1.2 %copy-start.1 = (s32[64,4096]{1,0:T(8,128)S(1)}, s32[64,4096]{1,0:T(8,128)}, u32[]{:S(2)}) copy-start(s32[64,4096]{1,0:T(8,128)} %ids_hbm.1) | copy-start | bytes 3145732

commit v3 on v2

--- a/solution.py
+++ b/solution.py
@@ -136,15 +136,21 @@
             slot = r * owners + mine
 
             def share(o, c):
-                to = lax.rem(me + o, devices)
+                for turn in range(m):
+                    pltpu.make_async_remote_copy(
+                        src_ref=pair_src.at[step], dst_ref=pair_dst.at[step, slot],
+                        send_sem=pair_send.at[step], recv_sem=pair_recv.at[step],
+                        device_id={"act": lax.rem(a + o, n), "rep": lax.rem(r + turn, m)}, device_id_type=MESH,
+                    ).start()
+                return c
+
+            lax.fori_loop(1, n, share, 0)
+            for turn in range(1, m):
                 pltpu.make_async_remote_copy(
                     src_ref=pair_src.at[step], dst_ref=pair_dst.at[step, slot],
                     send_sem=pair_send.at[step], recv_sem=pair_recv.at[step],
-                    device_id={"act": lax.rem(to, n), "rep": to // n}, device_id_type=MESH,
+                    device_id={"rep": lax.rem(r + turn, m)}, device_id_type=MESH,
                 ).start()
-                return c
-
-            lax.fori_loop(1, devices, share, 0)
             pair_dst[step, slot] = pair_src[step]
             all_but_one(pair_dst.at[step], owners * m, pair_recv.at[step])
 

time: 48.6 us -> 48.2 us (level)
  no operation moved by 1% of the time
where the time goes in v3:
time: 48.2 us; the launch traced here: 48 us
  Pallas kernels  43.6 us (90%)
  local copies, waits for them, and re-layouts  2.44 us (5%)
  between operations  1.94 us (4%)
    pallas_call x1, Pallas kernels, on_device(): pl.pallas_call(functools.partial(kernel, n, m), name='dual', out_shape=(j...  42.5 us
    unnamed x4, local copies, waits for them, and re-layouts  2.44 us
    pallas_call x1, Pallas kernels, on_device(): pl.pallas_call(finish, name='finish', out_shape=(jax.ShapeDtypeStruct((ro...  1.07 us

profile of v3, /device:TPU:0, one launch (start us, length us, event | category | flops | bytes accessed | tf_op | source)
XLA Modules:
  0.0 48.0 jit_solution(12017266548245066951)
XLA Ops:
  1.9 0.0 copy-start
  1.9 1.2 %copy-done = f32[64,4096]{1,0:T(8,128)S(1)} copy-done((f32[64,4096]{1,0:T(8,128)S(1)}, f32[64,4096]{1,0:T(8,128)}, u32[]{:S(2)}) %copy-start) | copy-done | bytes 1048600
  3.1 0.0 copy-start.1
  3.1 1.2 %copy-done.1 = s32[64,4096]{1,0:T(8,128)S(1)} copy-done((s32[64,4096]{1,0:T(8,128)S(1)}, s32[64,4096]{1,0:T(8,128)}, u32[]{:S(2)}) %copy-start.1) | copy-done | bytes 1048600
  4.4 42.5 %dual.1 = (f32[64,4096]{1,0:T(8,128)S(1)}, f32[1,4096]{1,0:T(1,128)S(1)}, f32[18,512]{1,0:T(8,128)S(1)}, f32[1,128]{1,0:T(1,128)S(1)}) custom-call(f32[64,4096]{1,0:T(8,128)S(1)} %copy-done, s32[64,4096]{1,0:T(8,128)S(1)} %copy-done.1, f32[1]{0:T(128)S(6)} %copy.7.eta_ref, f32[1]{0:T(128)S(6)} %copy.8.eps_ref), custom_call_target="tpu_custom_call" | custom-call | tf_op jit(solution)/shard_map/dual/pallas_call | solution.py:289
  46.9 1.1 %finish.1 = (f32[64,4096]{1,0:T(8,128)}, f32[18,512]{1,0:T(8,128)}, f32[1,128]{1,0:T(1,128)}) custom-call(f32[64,4096]{1,0:T(8,128)S(1)} %get-tuple-element.10.expo_ref, f32[1,4096]{1,0:T(1,128)S(1)} %get-tuple-element.11.scale_ref, f32[18,512]{1,0:T(8,128)S(1)} %get-tuple-element.12.goal_ref, f32[1,128]{1,0:T(1,128)S(1)} %get-tuple-element.13.eta_ref), custom_call_target="tpu_custom_call" | custom-call | tf_op jit(solution)/shard_map/finish/pallas_call | solution.py:321
Async XLA Ops:
  1.9 1.2 %copy-start = (f32[64,4096]{1,0:T(8,128)S(1)}, f32[64,4096]{1,0:T(8,128)}, u32[]{:S(2)}) copy-start(f32[64,4096]{1,0:T(8,128)} %q_hbm.1) | copy-start | bytes 3145732
  3.1 1.2 %copy-start.1 = (s32[64,4096]{1,0:T(8,128)S(1)}, s32[64,4096]{1,0:T(8,128)}, u32[]{:S(2)}) copy-start(s32[64,4096]{1,0:T(8,128)} %ids_hbm.1) | copy-start | bytes 3145732
